TPU v7x, 32 devices: a whole 2x2x4 slice. The times are simulated.
32 devices in a mesh: row: 8 (over y, x, core), col: 4 (over z).
Axes of the slice: x: 2, y: 2, z: 4, core: 2. Of those that a mesh axis runs over, the one named last changes fastest.
Arguments:
- right_side: float32 [2, 2048, 1024], P(None, 'row', 'col'), may hold values from -6 to 6
- probe: float32 [2, 256, 256], replicated, may hold values from -6 to 6
- detector_weights: float32 [256, 256], replicated, may hold values from 0.1 to 10
- offsets: int32 [8, 4, 4, 2], P('row', 'col'), may hold values from -128 to 127, as said below
- counts: int32 [8, 4], P('row', 'col'), may hold values from 2 to 4, as said below
Outputs:
- solution_field: float32 [2, 2048, 1024], P(None, 'row', 'col')
- residual: float32 [2, 2048, 1024], P(None, 'row', 'col')
Inputs may be any that keep to these rules, and one draw needn't show every extreme that they name: `counts`: every region holds at least two positions; in every draw some region holds exactly 4. In every region slot 0 has both offsets negative and slot 1 both offsets non-negative.
All inputs are finite; a program needn't handle non-finite values.
Results may differ from a plain program's by a relative error of at most 0.0003.
Values sent between devices are 32-bit elements; how exact they have to be, the bound alone decides.
A program may use at most 64 MiB of HBM per device.

v0:
```python
import functools
import math

import jax
import jax.numpy as jnp
import numpy as np
from jax import lax
from jax.experimental import pallas as pl
from jax.experimental.pallas import tpu as pltpu
from jax.sharding import PartitionSpec as P

ITERS = 3
RIDGE = 0.5
MESH = pl.DeviceIdType.MESH
F32 = jnp.float32
BF16 = jnp.bfloat16


def tables(length):
    half = length // 2
    k = np.arange(half)[:, None]
    n = np.arange(half)[None, :]
    out = []
    for odd in (0, 1):
        angle = 2.0 * math.pi * ((n * (2 * k + odd)) % length) / length
        re, im = np.cos(angle) / math.sqrt(length), -np.sin(angle) / math.sqrt(length)
        real = np.block([[re, -im], [im, re]])
        for mat in (real, real.T):
            hi = mat.astype(BF16)
            out += [hi, (mat - hi.astype(np.float64)).astype(BF16)]
    return np.stack(out)


def kernel(
    n_row, n_col, cap, side,
    off_ref, cnt_ref, rhs_ref, probe_ref, w_ref, mat_ref,
    sol_ref, res_ref,
    R, G, L, S, D, PR, X, Y, RB, CB, T, T1, T2,
    bar_send, bar_recv, s1_send, s1_recv, s2_send, s2_recv,
):
    h = side // 2
    own = slice(h, h + side)
    row = lax.axis_index("row")
    col = lax.axis_index("col")

    def chunks(total, step, body):
        def run(i, carry):
            body(pl.ds(pl.multiple_of(i * step, step), step), i * step)
            return carry
        lax.fori_loop(0, total // step, run, 0)

    def clear(rows, _):
        G[:, rows, :] = jnp.zeros((2, 32, 2 * side), F32)
    chunks(2 * side, 32, clear)

    def clear_b(rows, _):
        RB[:, :, rows, :] = jnp.zeros((2, 2, 32, 2 * side), F32)
    chunks(h, 32, clear_b)

    def clear_c(rows, _):
        CB[:, :, rows, :] = jnp.zeros((2, 2, 32, h), F32)
    chunks(side, 32, clear_c)
    G[:, own, own] = rhs_ref[...]

    barrier = pltpu.get_barrier_semaphore()
    for d in range(1, n_row):
        pl.semaphore_signal(barrier, inc=1, device_id=(lax.rem(row + d, n_row), col), device_id_type=MESH)
    for d in range(1, n_col):
        pl.semaphore_signal(barrier, inc=1, device_id=(row, lax.rem(col + d, n_col)), device_id_type=MESH)
    pl.semaphore_wait(barrier, n_row - 1 + n_col - 1)

    def both(index, low_src, low_dst, high_src, high_dst, axis):
        at, count = (row, n_row) if axis == 0 else (col, n_col)

        def target(step):
            return (row + step, col) if axis == 0 else (row, col + step)

        low = pltpu.make_async_remote_copy(
            src_ref=low_src, dst_ref=low_dst, send_sem=bar_send.at[2 * index], recv_sem=bar_recv.at[2 * index],
            device_id=target(-1), device_id_type=MESH)
        high = pltpu.make_async_remote_copy(
            src_ref=high_src, dst_ref=high_dst, send_sem=bar_send.at[2 * index + 1],
            recv_sem=bar_recv.at[2 * index + 1], device_id=target(1), device_id_type=MESH)

        def start():
            pl.when(at > 0)(low.start)
            pl.when(at < count - 1)(high.start)

        def wait():
            @pl.when(at > 0)
            def _():
                low.wait_send()
                high.wait_recv()

            @pl.when(at < count - 1)
            def _():
                high.wait_send()
                low.wait_recv()

        return start, wait

    def gather():
        start, wait = both(
            2, G.at[:, own, h:2 * h], G.at[:, own, 3 * h:4 * h], G.at[:, own, 2 * h:3 * h], G.at[:, own, 0:h], 1)
        start()
        wait()
        start, wait = both(
            3, G.at[:, h:2 * h, :], G.at[:, 3 * h:4 * h, :], G.at[:, 2 * h:3 * h, :], G.at[:, 0:h, :], 0)
        start()
        return wait

    gather_wait = gather()

    for s in range(cap):
        on = jnp.where(s < cnt_ref[0], 1.0, 0.0).astype(F32)
        for c in range(2):
            rolled = pltpu.roll(probe_ref[c], off_ref[2 * s] + h, 0)
            PR[s, c] = pltpu.roll(rolled, off_ref[2 * s + 1] + h, 1) * on

    gather_wait()

    def put(j, rows, val):
        hi = val.astype(BF16)
        X[j, 0, rows, :] = hi
        X[j, 1, rows, :] = (val - hi.astype(F32)).astype(BF16)

    def left(m, j):
        hi, lo = mat_ref[m], mat_ref[m + 1]
        xh, xl = X[j, 0], X[j, 1]
        return jnp.dot(jnp.concatenate([hi, lo, hi], 1), jnp.concatenate([xh, xh, xl], 0), preferred_element_type=F32)

    def right(j, m):
        hi, lo = mat_ref[m], mat_ref[m + 1]
        xh, xl = X[j, 0], X[j, 1]
        return jnp.dot(jnp.concatenate([xh, xl, xh], 1), jnp.concatenate([hi, hi, lo], 0), preferred_element_type=F32)

    step = 32

    def fold(val):
        return jnp.sum(val.reshape(-1, 8, val.shape[-1]), axis=0)

    def patch(s, acc):
        a = off_ref[2 * s] + h
        b = off_ref[2 * s + 1] + h
        ri = lax.broadcasted_iota(jnp.int32, (step, side), 0)
        in_col = lax.broadcasted_iota(jnp.int32, (step, side), 1) >= b
        for t in range(0, h, step):
            parts = []
            for base in (t, h + t):
                rows, far = slice(base, base + step), slice(side + base, side + base + step)
                in_row = ri + base >= a
                v = [
                    jnp.where(in_row, jnp.where(in_col, R[c, rows, 0:side], R[c, rows, side:]),
                              jnp.where(in_col, R[c, far, 0:side], R[c, far, side:]))
                    for c in range(2)
                ]
                p0, p1 = PR[s, 0, rows, :], PR[s, 1, rows, :]
                parts.append((p0 * v[0] - p1 * v[1], p0 * v[1] + p1 * v[0]))
            for c in range(2):
                rows = slice(c * h + t, c * h + t + step)
                put(0, rows, parts[0][c] + parts[1][c])
                put(1, rows, parts[0][c] - parts[1][c])
        Y[0] = left(0, 0)
        Y[1] = left(4, 1)
        for j in range(2):
            for t in range(0, h, step):
                re, im = Y[j, t:t + step, :], Y[j, h + t:h + t + step, :]
                rows = slice(j * h + t, j * h + t + step)
                put(2, rows, jnp.concatenate([re[:, :h] + re[:, h:], im[:, :h] + im[:, h:]], 1))
                put(3, rows, jnp.concatenate([re[:, :h] - re[:, h:], im[:, :h] - im[:, h:]], 1))
        Y[2] = right(2, 2)
        Y[3] = right(3, 6)
        for j in range(2):
            for t in range(0, side, step):
                rows = slice(t, t + step)
                f = Y[2 + j, rows, :]
                wf = w_ref[j, rows, :] * f
                acc = acc + fold(wf * f)
                put(j, rows, wf)
        Y[0] = right(0, 0)
        Y[1] = right(1, 4)
        for j in range(2):
            for t in range(0, h, step):
                rows = slice(j * h + t, j * h + t + step)
                c, d = Y[0, rows, :], Y[1, rows, :]
                p, m = c + d, c - d
                put(2 + j, slice(t, t + step), jnp.concatenate([p[:, :h], m[:, :h]], 1))
                put(2 + j, slice(h + t, h + t + step), jnp.concatenate([p[:, h:], m[:, h:]], 1))
        Y[2] = left(2, 2)
        Y[3] = left(6, 3)
        for t in range(0, h, step):
            for sign, base in ((1, t), (-1, h + t)):
                rows, far = slice(base, base + step), slice(side + base, side + base + step)
                hr = Y[2, t:t + step, :] + sign * Y[3, t:t + step, :]
                hi = Y[2, h + t:h + t + step, :] + sign * Y[3, h + t:h + t + step, :]
                p0, p1 = PR[s, 0, rows, :], PR[s, 1, rows, :]
                in_row = ri + base >= a
                for c, term in ((0, p0 * hr + p1 * hi), (1, p0 * hi - p1 * hr)):
                    near_r = jnp.where(in_row, term, 0.0)
                    far_r = term - near_r
                    nn = jnp.where(in_col, near_r, 0.0)
                    fn = jnp.where(in_col, far_r, 0.0)
                    S[c, rows, 0:side] += nn
                    S[c, rows, side:] += near_r - nn
                    S[c, far, 0:side] += fn
                    S[c, far, side:] += far_r - fn
        return acc

    def copy_r(rows, _):
        R[:, rows, :] = G[:, rows, :]
    chunks(2 * side, 32, copy_r)

    ti = lax.broadcasted_iota(jnp.int32, (8, 128), 0)

    def lanes(acc):
        total = acc[:, 0:128]
        for q in range(128, acc.shape[1], 128):
            total = total + acc[:, q:q + 128]
        return jnp.sum(total, axis=0, keepdims=True)

    alpha = rr_before = None
    for it in range(ITERS):
        last = it + 1 == ITERS

        def clear_s(rows, _):
            S[:, rows, :] = jnp.zeros((2, 32, 2 * side), F32)
        chunks(2 * side, 32, clear_s)

        def norm(i, acc):
            v = R[:, pl.ds(pl.multiple_of(h + i * 32, 32), 32), own]
            return acc + fold(v[0] * v[0]) + fold(v[1] * v[1])
        rr_acc = lax.fori_loop(0, side // 32, norm, jnp.zeros((8, side), F32))
        acc = lax.fori_loop(0, cap, patch, jnp.zeros((8, side), F32))

        rs_start, rs_wait = both(0, S.at[:, 0:h, :], RB.at[0], S.at[:, 3 * h:4 * h, :], RB.at[1], 0)
        rs_start()
        rr_l, pap_l = lanes(rr_acc), lanes(acc)
        T1[it, row] = jnp.where(ti == 0, rr_l, jnp.where(ti == 1, pap_l + RIDGE * rr_l, 0.0))
        ones = [
            pltpu.make_async_remote_copy(
                src_ref=T1.at[it, row], dst_ref=T1.at[it, row], send_sem=s1_send.at[it, d],
                recv_sem=s1_recv.at[it, d], device_id=(lax.rem(row + d, n_row), col), device_id_type=MESH)
            for d in range(1, n_row)
        ]
        for copy in ones:
            copy.start()
        rs_wait()

        def add_rows(i, carry):
            near = pl.ds(pl.multiple_of(i * 32, 32), 32)
            top = pl.ds(pl.multiple_of(h + i * 32, 32), 32)
            bottom = pl.ds(pl.multiple_of(2 * h + i * 32, 32), 32)
            S[:, top, :] += RB[1, :, near, :]
            S[:, bottom, :] += RB[0, :, near, :]
            return carry
        lax.fori_loop(0, h // 32, add_rows, 0)
        cs_start, cs_wait = both(1, S.at[:, own, 0:h], CB.at[0], S.at[:, own, 3 * h:4 * h], CB.at[1], 1)
        cs_start()
        for copy in ones:
            copy.wait()
        total = T1[it, 0]
        for q in range(1, n_row):
            total = total + T1[it, q]
        T2[it, col] = total
        twos = [
            pltpu.make_async_remote_copy(
                src_ref=T2.at[it, col], dst_ref=T2.at[it, col], send_sem=s2_send.at[it, d],
                recv_sem=s2_recv.at[it, d], device_id=(row, lax.rem(col + d, n_col)), device_id_type=MESH)
            for d in range(1, n_col)
        ]
        for copy in twos:
            copy.start()
        cs_wait()

        def make_image(i, carry):
            rows = pl.ds(pl.multiple_of(h + i * 32, 32), 32)
            near = pl.ds(pl.multiple_of(i * 32, 32), 32)
            G[:, rows, h:2 * h] = S[:, rows, h:2 * h] + CB[1, :, near, :] + RIDGE * R[:, rows, h:2 * h]
            G[:, rows, 2 * h:3 * h] = S[:, rows, 2 * h:3 * h] + CB[0, :, near, :] + RIDGE * R[:, rows, 2 * h:3 * h]
            return carry
        lax.fori_loop(0, side // 32, make_image, 0)
        gather_wait = None if last else gather()
        for copy in twos:
            copy.wait()
        total = T2[it, 0]
        for q in range(1, n_col):
            total = total + T2[it, q]
        rr = jnp.sum(jnp.where(ti == 0, total, 0.0), keepdims=True)
        pap = jnp.sum(jnp.where(ti == 1, total, 0.0), keepdims=True)
        if it == 0:
            ratio = None
            alpha = rr / pap
        else:
            ratio = rr / rr_before
            alpha = rr / (pap - ratio * rr / alpha)
        rr_before = rr

        def advance(i, carry):
            near = pl.ds(pl.multiple_of(i * 32, 32), 32)
            rows = pl.ds(pl.multiple_of(h + i * 32, 32), 32)
            for c in range(2):
                r = R[c, rows, own]
                d = r if it == 0 else r + ratio * D[c, near, :]
                if not last:
                    D[c, near, :] = d
                sol_ref[c, near, :] = alpha * d if it == 0 else sol_ref[c, near, :] + alpha * d
                if last:
                    along = G[c, rows, own] + ratio * L[c, rows, own]
                    res_ref[c, near, :] = r - alpha * along
            return carry
        lax.fori_loop(0, side // 32, advance, 0)
        if not last:
            gather_wait()

            def advance_r(rows, _):
                for c in range(2):
                    along = G[c, rows, :] if it == 0 else G[c, rows, :] + ratio * L[c, rows, :]
                    L[c, rows, :] = along
                    R[c, rows, :] = R[c, rows, :] - alpha * along
            chunks(2 * side, 32, advance_r)


def solution(mesh):
    n_row, n_col = mesh.shape["row"], mesh.shape["col"]

    def local(right_side, probe, weights, offsets, counts):
        side = probe.shape[1]
        cap = offsets.shape[2]
        h = side // 2
        mats = jnp.asarray(tables(side))
        by_row = jnp.concatenate([weights[0::2], weights[1::2]], axis=0)
        w = jnp.stack([jnp.concatenate([by_row[:, q::2]] * 2, axis=1) for q in range(2)])
        block = jax.ShapeDtypeStruct((2, side, side), F32)
        vmem = pl.BlockSpec(memory_space=pltpu.VMEM)
        smem = pl.BlockSpec(memory_space=pltpu.SMEM)
        wide = pltpu.VMEM((2, 2 * side, 2 * side), F32)
        dma = pltpu.SemaphoreType.DMA
        return pl.pallas_call(
            functools.partial(kernel, n_row, n_col, cap, side),
            out_shape=(block, block),
            in_specs=[smem, smem, vmem, vmem, vmem, vmem],
            out_specs=(vmem, vmem),
            scratch_shapes=[
                wide, wide, wide, wide,
                pltpu.VMEM((2, side, side), F32),
                pltpu.VMEM((cap, 2, side, side), F32),
                pltpu.VMEM((4, 2, side, side), BF16),
                pltpu.VMEM((4, side, side), F32),
                pltpu.VMEM((2, 2, h, 2 * side), F32),
                pltpu.VMEM((2, 2, side, h), F32),
                pltpu.VMEM((8, 128), F32),
                pltpu.VMEM((ITERS, n_row, 8, 128), F32),
                pltpu.VMEM((ITERS, n_col, 8, 128), F32),
                dma((8,)), dma((8,)),
                dma((ITERS, n_row)), dma((ITERS, n_row)),
                dma((ITERS, n_col)), dma((ITERS, n_col)),
            ],
            compiler_params=pltpu.CompilerParams(
                collective_id=0, has_side_effects=True, vmem_limit_bytes=48 * 1024 * 1024),
        )(offsets.reshape(-1), counts.reshape(-1), right_side, probe, w, mats)

    placed = (P(None, "row", "col"), P(), P(), P("row", "col", None, None), P("row", "col"))
    return jax.shard_map(
        local, mesh=mesh, in_specs=placed, out_specs=(P(None, "row", "col"), P(None, "row", "col")), check_vma=False)
```

profile of v0, /device:TPU:0, one launch (start us, length us, event | category | flops | bytes accessed | tf_op | source)
XLA Modules:
  0.0 153.4 jit_solution(9806505644043103097)
XLA Ops:
  0.6 0.0 copy-start.3
  1.3 0.8 copy.9
  2.1 0.1 reshape.10.off_ref
  2.2 1.0 slice.13
  3.2 0.0 copy-done.3
  3.2 0.1 slice.12
  3.3 4.5 %slice.15 = f32[256,128]{1,0:T(8,128)S(1)} slice(f32[256,256]{1,0:T(8,128)S(1)} %pad_maximum_fusion.1), slice={[0:256:1], [1:256:2]} | slice | bytes 262144 | tf_op jit(solution)/shard_map/slice | solution.py:332
  7.8 0.0 copy-start
  7.8 4.5 %slice.14 = f32[256,128]{1,0:T(8,128)S(1)} slice(f32[256,256]{1,0:T(8,128)S(1)} %pad_maximum_fusion.1), slice={[0:256:1], [0:256:2]} | slice | bytes 262144 | tf_op jit(solution)/shard_map/slice | solution.py:332
  12.4 0.0 copy-start.1
  12.4 0.0 copy-start.2
  12.5 0.0 copy-done
  12.5 1.0 copy-done.1
  13.4 0.2 copy-done.2
  13.6 138.2 %shard_map.77 = (f32[2,256,256]{2,1,0:T(8,128)S(1)}, f32[2,256,256]{2,1,0:T(8,128)S(1)}) custom-call(s32[8]{0:T(128)S(1)} %reshape.10.off_ref, s32[1]{0:T(128)} %bitcast.5.cnt_ref, f32[2,256,256]{2,1,0:T(8,128)S(1)} %copy-done.1, f32[2,256,256]{2,1,0:T(8,128)S(1)} %copy-done.2, f32[2,256,256]{2,1,0:T(8,128)S(1)} %pad_maximum_fusion.w_ref, ...), custom_call_target="tpu_custom_call" | custom-call | tf_op jit(solution)/shard_map/pallas_call | solution.py:338
  151.8 0.8 copy.13
  152.6 0.8 copy.14
  (3 shorter events, 0.1 us)
Async XLA Ops:
  0.6 2.6 %copy-start.3 = (f32[256,256]{1,0:T(8,128)S(1)}, f32[256,256]{1,0:T(8,128)}, u32[]{:S(2)}) copy-start(f32[256,256]{1,0:T(8,128)} %param.8) | copy-start | bytes 786436
  7.8 4.6 %copy-start = (bf16[8,256,256]{2,1,0:T(8,128)(2,1)S(1)}, bf16[8,256,256]{2,1,0:T(8,128)(2,1)}, u32[]{:S(2)}) copy-start(bf16[8,256,256]{2,1,0:T(8,128)(2,1)} %constant.2.clone.mat_ref) | copy-start | bytes 3145732
  12.4 1.0 copy-start.1
  12.4 1.2 copy-start.2
where the time goes:
time: 155 us; the launch traced here: 153 us
  Pallas kernels  138 us (89%)
  local copies, waits for them, and re-layouts  13.7 us (9%)
    pallas_call x1, Pallas kernels, local(): pl.pallas_call(functools.partial(kernel, n_row, n_col, cap, side), out_sh...  138 us
    slice x2, local copies, waits for them, and re-layouts, local(): by_row[:, q::2]  8.98 us
    unnamed x11, local copies, waits for them, and re-layouts  3.5 us

commit v1 on v0

--- a/solution.py
+++ b/solution.py
@@ -35,7 +35,7 @@
     n_row, n_col, cap, side,
     off_ref, cnt_ref, rhs_ref, probe_ref, w_ref, mat_ref,
     sol_ref, res_ref,
-    R, G, L, S, D, PR, X, Y, RB, CB, T, T1, T2,
+    R, G, L, S, D, PR, X, Y, W, RA, CA, CC, RC, T1, T2,
     bar_send, bar_recv, s1_send, s1_recv, s2_send, s2_recv,
 ):
     h = side // 2
@@ -53,13 +53,10 @@
         G[:, rows, :] = jnp.zeros((2, 32, 2 * side), F32)
     chunks(2 * side, 32, clear)
 
-    def clear_b(rows, _):
-        RB[:, :, rows, :] = jnp.zeros((2, 2, 32, 2 * side), F32)
-    chunks(h, 32, clear_b)
-
-    def clear_c(rows, _):
-        CB[:, :, rows, :] = jnp.zeros((2, 2, 32, h), F32)
-    chunks(side, 32, clear_c)
+    for buf in (RA, CA, CC, RC):
+        def clear_b(rows, _, buf=buf):
+            buf[:, rows, :] = jnp.zeros((2, 32, buf.shape[2]), F32)
+        chunks(buf.shape[1], 32, clear_b)
     G[:, own, own] = rhs_ref[...]
 
     barrier = pltpu.get_barrier_semaphore()
@@ -100,13 +97,25 @@
         return start, wait
 
     def gather():
-        start, wait = both(
-            2, G.at[:, own, h:2 * h], G.at[:, own, 3 * h:4 * h], G.at[:, own, 2 * h:3 * h], G.at[:, own, 0:h], 1)
-        start()
-        wait()
-        start, wait = both(
-            3, G.at[:, h:2 * h, :], G.at[:, 3 * h:4 * h, :], G.at[:, 2 * h:3 * h, :], G.at[:, 0:h, :], 0)
-        start()
+        re_start, re_wait = both(
+            4, G.at[0, own, h:2 * h], G.at[0, own, 3 * h:4 * h], G.at[0, own, 2 * h:3 * h], G.at[0, own, 0:h], 1)
+        im_start, im_wait = both(
+            5, G.at[1, h:2 * h, own], G.at[1, 3 * h:4 * h, own], G.at[1, 2 * h:3 * h, own], G.at[1, 0:h, own], 0)
+        re_start()
+        im_start()
+        re_wait()
+        re_start, re_wait = both(
+            6, G.at[0, h:2 * h, :], G.at[0, 3 * h:4 * h, :], G.at[0, 2 * h:3 * h, :], G.at[0, 0:h, :], 0)
+        re_start()
+        im_wait()
+        im_start, im_wait = both(
+            7, G.at[1, :, h:2 * h], G.at[1, :, 3 * h:4 * h], G.at[1, :, 2 * h:3 * h], G.at[1, :, 0:h], 1)
+        im_start()
+
+        def wait():
+            re_wait()
+            im_wait()
+
         return wait
 
     gather_wait = gather()
@@ -116,6 +125,27 @@
         for c in range(2):
             rolled = pltpu.roll(probe_ref[c], off_ref[2 * s] + h, 0)
             PR[s, c] = pltpu.roll(rolled, off_ref[2 * s + 1] + h, 1) * on
+
+    def three(val):
+        top = val.astype(BF16)
+        rest = val - top.astype(F32)
+        mid = rest.astype(BF16)
+        return top, mid, (rest - mid.astype(F32)).astype(BF16)
+
+    first = lax.broadcasted_iota(jnp.int32, (side, side), 0)
+    second = lax.broadcasted_iota(jnp.int32, (side, side), 1)
+    freq = jnp.where(first >= h, 2 * (first - h) + 1, 2 * first)
+    pick = jnp.where(second == freq, 1.0, 0.0).astype(BF16)
+    by_row = sum(jnp.dot(pick, part, preferred_element_type=F32) for part in three(w_ref[...]))
+    parts = three(by_row)
+    lane = jnp.where(second >= h, second - h, second)
+    for q in range(2):
+        pick = jnp.where(first == 2 * lane + q, 1.0, 0.0).astype(BF16)
+        W[q] = sum(jnp.dot(part, pick, preferred_element_type=F32) for part in parts)
+
+    def clear_s(rows, _):
+        S[:, rows, :] = jnp.zeros((2, 32, 2 * side), F32)
+    chunks(2 * side, 32, clear_s)
 
     gather_wait()
 
@@ -174,7 +204,7 @@
             for t in range(0, side, step):
                 rows = slice(t, t + step)
                 f = Y[2 + j, rows, :]
-                wf = w_ref[j, rows, :] * f
+                wf = W[j, rows, :] * f
                 acc = acc + fold(wf * f)
                 put(j, rows, wf)
         Y[0] = right(0, 0)
@@ -222,18 +252,16 @@
     for it in range(ITERS):
         last = it + 1 == ITERS
 
-        def clear_s(rows, _):
-            S[:, rows, :] = jnp.zeros((2, 32, 2 * side), F32)
-        chunks(2 * side, 32, clear_s)
-
         def norm(i, acc):
             v = R[:, pl.ds(pl.multiple_of(h + i * 32, 32), 32), own]
             return acc + fold(v[0] * v[0]) + fold(v[1] * v[1])
         rr_acc = lax.fori_loop(0, side // 32, norm, jnp.zeros((8, side), F32))
         acc = lax.fori_loop(0, cap, patch, jnp.zeros((8, side), F32))
 
-        rs_start, rs_wait = both(0, S.at[:, 0:h, :], RB.at[0], S.at[:, 3 * h:4 * h, :], RB.at[1], 0)
-        rs_start()
+        re_start, re_wait = both(0, S.at[0, 0:h, :], RA.at[0], S.at[0, 3 * h:4 * h, :], RA.at[1], 0)
+        im_start, im_wait = both(1, S.at[1, :, 0:h], CC.at[0], S.at[1, :, 3 * h:4 * h], CC.at[1], 1)
+        re_start()
+        im_start()
         rr_l, pap_l = lanes(rr_acc), lanes(acc)
         T1[it, row] = jnp.where(ti == 0, rr_l, jnp.where(ti == 1, pap_l + RIDGE * rr_l, 0.0))
         ones = [
@@ -244,18 +272,26 @@
         ]
         for copy in ones:
             copy.start()
-        rs_wait()
+        re_wait()
 
         def add_rows(i, carry):
             near = pl.ds(pl.multiple_of(i * 32, 32), 32)
             top = pl.ds(pl.multiple_of(h + i * 32, 32), 32)
             bottom = pl.ds(pl.multiple_of(2 * h + i * 32, 32), 32)
-            S[:, top, :] += RB[1, :, near, :]
-            S[:, bottom, :] += RB[0, :, near, :]
+            S[0, top, :] += RA[1, near, :]
+            S[0, bottom, :] += RA[0, near, :]
             return carry
         lax.fori_loop(0, h // 32, add_rows, 0)
-        cs_start, cs_wait = both(1, S.at[:, own, 0:h], CB.at[0], S.at[:, own, 3 * h:4 * h], CB.at[1], 1)
-        cs_start()
+        re_start, re_wait = both(2, S.at[0, own, 0:h], CA.at[0], S.at[0, own, 3 * h:4 * h], CA.at[1], 1)
+        re_start()
+        im_wait()
+
+        def add_cols(rows, _):
+            S[1, rows, h:2 * h] += CC[1, rows, :]
+            S[1, rows, 2 * h:3 * h] += CC[0, rows, :]
+        chunks(2 * side, 32, add_cols)
+        im_start, im_wait = both(3, S.at[1, 0:h, own], RC.at[0], S.at[1, 3 * h:4 * h, own], RC.at[1], 0)
+        im_start()
         for copy in ones:
             copy.wait()
         total = T1[it, 0]
@@ -270,15 +306,24 @@
         ]
         for copy in twos:
             copy.start()
-        cs_wait()
-
-        def make_image(i, carry):
+        re_wait()
+
+        def make_re(i, carry):
             rows = pl.ds(pl.multiple_of(h + i * 32, 32), 32)
             near = pl.ds(pl.multiple_of(i * 32, 32), 32)
-            G[:, rows, h:2 * h] = S[:, rows, h:2 * h] + CB[1, :, near, :] + RIDGE * R[:, rows, h:2 * h]
-            G[:, rows, 2 * h:3 * h] = S[:, rows, 2 * h:3 * h] + CB[0, :, near, :] + RIDGE * R[:, rows, 2 * h:3 * h]
+            G[0, rows, h:2 * h] = S[0, rows, h:2 * h] + CA[1, near, :] + RIDGE * R[0, rows, h:2 * h]
+            G[0, rows, 2 * h:3 * h] = S[0, rows, 2 * h:3 * h] + CA[0, near, :] + RIDGE * R[0, rows, 2 * h:3 * h]
             return carry
-        lax.fori_loop(0, side // 32, make_image, 0)
+        lax.fori_loop(0, side // 32, make_re, 0)
+        im_wait()
+
+        def make_im(i, carry):
+            near = pl.ds(pl.multiple_of(i * 32, 32), 32)
+            for q in range(2):
+                rows = pl.ds(pl.multiple_of((1 + q) * h + i * 32, 32), 32)
+                G[1, rows, own] = S[1, rows, own] + RC[1 - q, near, :] + RIDGE * R[1, rows, own]
+            return carry
+        lax.fori_loop(0, h // 32, make_im, 0)
         gather_wait = None if last else gather()
         for copy in twos:
             copy.wait()
@@ -310,6 +355,7 @@
             return carry
         lax.fori_loop(0, side // 32, advance, 0)
         if not last:
+            chunks(2 * side, 32, clear_s)
             gather_wait()
 
             def advance_r(rows, _):
@@ -328,8 +374,6 @@
         cap = offsets.shape[2]
         h = side // 2
         mats = jnp.asarray(tables(side))
-        by_row = jnp.concatenate([weights[0::2], weights[1::2]], axis=0)
-        w = jnp.stack([jnp.concatenate([by_row[:, q::2]] * 2, axis=1) for q in range(2)])
         block = jax.ShapeDtypeStruct((2, side, side), F32)
         vmem = pl.BlockSpec(memory_space=pltpu.VMEM)
         smem = pl.BlockSpec(memory_space=pltpu.SMEM)
@@ -346,18 +390,20 @@
                 pltpu.VMEM((cap, 2, side, side), F32),
                 pltpu.VMEM((4, 2, side, side), BF16),
                 pltpu.VMEM((4, side, side), F32),
-                pltpu.VMEM((2, 2, h, 2 * side), F32),
-                pltpu.VMEM((2, 2, side, h), F32),
-                pltpu.VMEM((8, 128), F32),
+                pltpu.VMEM((2, side, side), F32),
+                pltpu.VMEM((2, h, 2 * side), F32),
+                pltpu.VMEM((2, side, h), F32),
+                pltpu.VMEM((2, 2 * side, h), F32),
+                pltpu.VMEM((2, h, side), F32),
                 pltpu.VMEM((ITERS, n_row, 8, 128), F32),
                 pltpu.VMEM((ITERS, n_col, 8, 128), F32),
-                dma((8,)), dma((8,)),
+                dma((16,)), dma((16,)),
                 dma((ITERS, n_row)), dma((ITERS, n_row)),
                 dma((ITERS, n_col)), dma((ITERS, n_col)),
             ],
             compiler_params=pltpu.CompilerParams(
                 collective_id=0, has_side_effects=True, vmem_limit_bytes=48 * 1024 * 1024),
-        )(offsets.reshape(-1), counts.reshape(-1), right_side, probe, w, mats)
+        )(offsets.reshape(-1), counts.reshape(-1), right_side, probe, weights, mats)
 
     placed = (P(None, "row", "col"), P(), P(), P("row", "col", None, None), P("row", "col"))
     return jax.shard_map(

time: 155 us -> 110 us (0.71)
  Pallas kernels: 138 us -> 102 us
  local copies, waits for them, and re-layouts: 13.7 us -> 6.7 us
    pallas_call x1, Pallas kernels: 138 us -> 102 us  [local(): pl.pallas_call(functools.partial(kernel, n_row, n_col, cap, side), out_sh...]
    slice x4 -> x0, local copies, waits for them, and re-layouts: 10.1 us -> none  [the longest x2 8.98 us: local(): by_row[:, q::2]]
    unnamed x11 -> x13, local copies, waits for them, and re-layouts: 3.5 us -> 6.61 us
where the time goes in v1:
time: 110 us
  Pallas kernels  102 us (93%)
  local copies, waits for them, and re-layouts  6.7 us (6%)
  between operations  1.3 us (1%)
    pallas_call x1, Pallas kernels, local(): pl.pallas_call(functools.partial(kernel, n_row, n_col, cap, side), out_sh...  102 us
    unnamed x13, local copies, waits for them, and re-layouts  6.61 us

profile of v1, /device:TPU:0, one launch (start us, length us, event | category | flops | bytes accessed | tf_op | source)
XLA Modules:
  0.0 109.8 jit_solution(7127880976913426099)
XLA Ops:
  1.3 0.0 copy-start.4
  1.3 0.7 copy-done.4
  2.0 0.1 copy.9
  2.0 0.1 reshape.10.off_ref
  2.1 0.0 copy-start
  2.1 1.2 %copy-done = bf16[8,256,256]{2,1,0:T(8,128)(2,1)S(1)} copy-done((bf16[8,256,256]{2,1,0:T(8,128)(2,1)S(1)}, bf16[8,256,256]{2,1,0:T(8,128)(2,1)}, u32[]{:S(2)}) %copy-start) | copy-done | bytes 1048600
  3.4 0.0 copy-start.1
  3.4 1.0 copy-done.1
  4.4 0.0 copy-start.2
  4.4 1.0 copy-done.2
  5.4 0.0 copy-start.3
  5.4 0.9 copy-done.3
  6.4 101.8 %shard_map.77 = (f32[2,256,256]{2,1,0:T(8,128)S(1)}, f32[2,256,256]{2,1,0:T(8,128)S(1)}) custom-call(s32[8]{0:T(128)S(1)} %reshape.10.off_ref, s32[1]{0:T(128)} %bitcast.1.cnt_ref, f32[2,256,256]{2,1,0:T(8,128)S(1)} %copy-done.1, f32[2,256,256]{2,1,0:T(8,128)S(1)} %copy-done.2, f32[256,256]{1,0:T(8,128)S(1)} %copy-done.3, bf16[8,256,256]{2,1,0:T(8,128)(2,1)S(1)} %copy-done), custom_call_target="tpu_custom_call" | custom-call | tf_op jit(solution)/shard_map/pallas_call | solution.py:382
  108.2 0.8 copy.13
  109.0 0.8 copy.14
Async XLA Ops:
  1.3 0.7 copy-start.4
  2.1 1.2 %copy-start = (bf16[8,256,256]{2,1,0:T(8,128)(2,1)S(1)}, bf16[8,256,256]{2,1,0:T(8,128)(2,1)}, u32[]{:S(2)}) copy-start(bf16[8,256,256]{2,1,0:T(8,128)(2,1)} %constant.2.clone.mat_ref) | copy-start | bytes 3145732
  3.4 1.0 copy-start.1
  4.4 1.0 copy-start.2
  5.4 0.9 copy-start.3

commit v2 on v1

--- a/solution.py
+++ b/solution.py
@@ -96,25 +96,30 @@
 
         return start, wait
 
+    edges = (slice(0, h), slice(3 * h, 4 * h))
+    one, two, top_h, end_h = slice(h, 2 * h), slice(2 * h, 3 * h), slice(0, h), slice(3 * h, 4 * h)
+
     def gather():
-        re_start, re_wait = both(
-            4, G.at[0, own, h:2 * h], G.at[0, own, 3 * h:4 * h], G.at[0, own, 2 * h:3 * h], G.at[0, own, 0:h], 1)
-        im_start, im_wait = both(
-            5, G.at[1, h:2 * h, own], G.at[1, 3 * h:4 * h, own], G.at[1, 2 * h:3 * h, own], G.at[1, 0:h, own], 0)
-        re_start()
-        im_start()
-        re_wait()
-        re_start, re_wait = both(
-            6, G.at[0, h:2 * h, :], G.at[0, 3 * h:4 * h, :], G.at[0, 2 * h:3 * h, :], G.at[0, 0:h, :], 0)
-        re_start()
-        im_wait()
-        im_start, im_wait = both(
-            7, G.at[1, :, h:2 * h], G.at[1, :, 3 * h:4 * h], G.at[1, :, 2 * h:3 * h], G.at[1, :, 0:h], 1)
-        im_start()
+        re_turn = both(8, G.at[0, own, one], G.at[0, own, end_h], G.at[0, own, two], G.at[0, own, top_h], 1)
+        im_turn = both(9, G.at[1, one, own], G.at[1, end_h, own], G.at[1, two, own], G.at[1, top_h, own], 0)
+        rest = [
+            both(10, G.at[0, one, own], G.at[0, end_h, own], G.at[0, two, own], G.at[0, top_h, own], 0),
+            both(11, G.at[1, own, one], G.at[1, own, end_h], G.at[1, own, two], G.at[1, own, top_h], 1),
+        ]
+        for start, _ in (re_turn, im_turn, *rest):
+            start()
+        re_turn[1]()
+        for q, e in enumerate(edges):
+            rest.append(both(12 + q, G.at[0, one, e], G.at[0, end_h, e], G.at[0, two, e], G.at[0, top_h, e], 0))
+            rest[-1][0]()
+        im_turn[1]()
+        for q, e in enumerate(edges):
+            rest.append(both(14 + q, G.at[1, e, one], G.at[1, e, end_h], G.at[1, e, two], G.at[1, e, top_h], 1))
+            rest[-1][0]()
 
         def wait():
-            re_wait()
-            im_wait()
+            for _, done in rest:
+                done()
 
         return wait
 
@@ -258,10 +263,18 @@
         rr_acc = lax.fori_loop(0, side // 32, norm, jnp.zeros((8, side), F32))
         acc = lax.fori_loop(0, cap, patch, jnp.zeros((8, side), F32))
 
-        re_start, re_wait = both(0, S.at[0, 0:h, :], RA.at[0], S.at[0, 3 * h:4 * h, :], RA.at[1], 0)
-        im_start, im_wait = both(1, S.at[1, :, 0:h], CC.at[0], S.at[1, :, 3 * h:4 * h], CC.at[1], 1)
-        re_start()
-        im_start()
+        re_edge = [
+            both(q, S.at[0, top_h, e], RA.at[0, :, e], S.at[0, end_h, e], RA.at[1, :, e], 0)
+            for q, e in enumerate(edges)
+        ]
+        im_edge = [
+            both(2 + q, S.at[1, e, top_h], CC.at[0, e, :], S.at[1, e, end_h], CC.at[1, e, :], 1)
+            for q, e in enumerate(edges)
+        ]
+        re_mid = both(4, S.at[0, top_h, own], RA.at[0, :, own], S.at[0, end_h, own], RA.at[1, :, own], 0)
+        im_mid = both(5, S.at[1, own, top_h], CC.at[0, own, :], S.at[1, own, end_h], CC.at[1, own, :], 1)
+        for start, _ in (*re_edge, *im_edge, re_mid, im_mid):
+            start()
         rr_l, pap_l = lanes(rr_acc), lanes(acc)
         T1[it, row] = jnp.where(ti == 0, rr_l, jnp.where(ti == 1, pap_l + RIDGE * rr_l, 0.0))
         ones = [
@@ -272,26 +285,31 @@
         ]
         for copy in ones:
             copy.start()
-        re_wait()
+        for _, done in re_edge:
+            done()
 
         def add_rows(i, carry):
             near = pl.ds(pl.multiple_of(i * 32, 32), 32)
-            top = pl.ds(pl.multiple_of(h + i * 32, 32), 32)
-            bottom = pl.ds(pl.multiple_of(2 * h + i * 32, 32), 32)
-            S[0, top, :] += RA[1, near, :]
-            S[0, bottom, :] += RA[0, near, :]
+            for q in range(2):
+                rows = pl.ds(pl.multiple_of((1 + q) * h + i * 32, 32), 32)
+                for e in edges:
+                    S[0, rows, e] += RA[1 - q, near, e]
             return carry
         lax.fori_loop(0, h // 32, add_rows, 0)
-        re_start, re_wait = both(2, S.at[0, own, 0:h], CA.at[0], S.at[0, own, 3 * h:4 * h], CA.at[1], 1)
-        re_start()
-        im_wait()
-
-        def add_cols(rows, _):
-            S[1, rows, h:2 * h] += CC[1, rows, :]
-            S[1, rows, 2 * h:3 * h] += CC[0, rows, :]
-        chunks(2 * side, 32, add_cols)
-        im_start, im_wait = both(3, S.at[1, 0:h, own], RC.at[0], S.at[1, 3 * h:4 * h, own], RC.at[1], 0)
-        im_start()
+        re_turn = both(6, S.at[0, own, top_h], CA.at[0], S.at[0, own, end_h], CA.at[1], 1)
+        re_turn[0]()
+        for _, done in im_edge:
+            done()
+
+        def add_cols(i, carry):
+            for base in (0, 3 * h):
+                rows = pl.ds(pl.multiple_of(base + i * 32, 32), 32)
+                S[1, rows, one] += CC[1, rows, :]
+                S[1, rows, two] += CC[0, rows, :]
+            return carry
+        lax.fori_loop(0, h // 32, add_cols, 0)
+        im_turn = both(7, S.at[1, top_h, own], RC.at[0], S.at[1, end_h, own], RC.at[1], 0)
+        im_turn[0]()
         for copy in ones:
             copy.wait()
         total = T1[it, 0]
@@ -306,24 +324,24 @@
         ]
         for copy in twos:
             copy.start()
-        re_wait()
-
-        def make_re(i, carry):
-            rows = pl.ds(pl.multiple_of(h + i * 32, 32), 32)
-            near = pl.ds(pl.multiple_of(i * 32, 32), 32)
-            G[0, rows, h:2 * h] = S[0, rows, h:2 * h] + CA[1, near, :] + RIDGE * R[0, rows, h:2 * h]
-            G[0, rows, 2 * h:3 * h] = S[0, rows, 2 * h:3 * h] + CA[0, near, :] + RIDGE * R[0, rows, 2 * h:3 * h]
-            return carry
-        lax.fori_loop(0, side // 32, make_re, 0)
-        im_wait()
-
-        def make_im(i, carry):
+        re_mid[1]()
+        im_mid[1]()
+        re_turn[1]()
+        im_turn[1]()
+
+        def make(i, carry):
             near = pl.ds(pl.multiple_of(i * 32, 32), 32)
             for q in range(2):
                 rows = pl.ds(pl.multiple_of((1 + q) * h + i * 32, 32), 32)
-                G[1, rows, own] = S[1, rows, own] + RC[1 - q, near, :] + RIDGE * R[1, rows, own]
+                inner = pl.ds(pl.multiple_of(q * h + i * 32, 32), 32)
+                re = S[0, rows, own] + RA[1 - q, near, own] + RIDGE * R[0, rows, own]
+                im = S[1, rows, own] + RC[1 - q, near, :] + RIDGE * R[1, rows, own]
+                G[0, rows, one] = re[:, :h] + CA[1, inner, :]
+                G[0, rows, two] = re[:, h:] + CA[0, inner, :]
+                G[1, rows, one] = im[:, :h] + CC[1, rows, :]
+                G[1, rows, two] = im[:, h:] + CC[0, rows, :]
             return carry
-        lax.fori_loop(0, h // 32, make_im, 0)
+        lax.fori_loop(0, h // 32, make, 0)
         gather_wait = None if last else gather()
         for copy in twos:
             copy.wait()
@@ -397,7 +415,7 @@
                 pltpu.VMEM((2, h, side), F32),
                 pltpu.VMEM((ITERS, n_row, 8, 128), F32),
                 pltpu.VMEM((ITERS, n_col, 8, 128), F32),
-                dma((16,)), dma((16,)),
+                dma((32,)), dma((32,)),
                 dma((ITERS, n_row)), dma((ITERS, n_row)),
                 dma((ITERS, n_col)), dma((ITERS, n_col)),
             ],

time: 110 us -> 103 us (0.936)
  Pallas kernels: 102 us -> 94.3 us
    pallas_call x1, Pallas kernels: 102 us -> 94.3 us  [local(): pl.pallas_call(functools.partial(kernel, n_row, n_col, cap, side), out_sh...]
where the time goes in v2:
time: 103 us; the launch traced here: 102 us
  Pallas kernels  94.3 us (92%)
  local copies, waits for them, and re-layouts  6.7 us (7%)
  between operations  1.3 us (1%)
    pallas_call x1, Pallas kernels, local(): pl.pallas_call(functools.partial(kernel, n_row, n_col, cap, side), out_sh...  94.3 us
    unnamed x13, local copies, waits for them, and re-layouts  6.61 us

profile of v2, /device:TPU:0, one launch (start us, length us, event | category | flops | bytes accessed | tf_op | source)
XLA Modules:
  0.0 102.2 jit_solution(8768271720397954846)
XLA Ops:
  1.3 0.0 copy-start.4
  1.3 0.7 copy-done.4
  2.0 0.1 copy.9
  2.0 0.1 reshape.10.off_ref
  2.1 0.0 copy-start
  2.1 1.2 %copy-done = bf16[8,256,256]{2,1,0:T(8,128)(2,1)S(1)} copy-done((bf16[8,256,256]{2,1,0:T(8,128)(2,1)S(1)}, bf16[8,256,256]{2,1,0:T(8,128)(2,1)}, u32[]{:S(2)}) %copy-start) | copy-done | bytes 1048600
  3.4 0.0 copy-start.1
  3.4 1.0 %copy-done.1 = f32[2,256,256]{2,1,0:T(8,128)S(1)} copy-done((f32[2,256,256]{2,1,0:T(8,128)S(1)}, f32[2,256,256]{2,1,0:T(8,128)}, u32[]{:S(2)}) %copy-start.1) | copy-done | bytes 524312
  4.4 0.0 copy-start.2
  4.4 1.0 %copy-done.2 = f32[2,256,256]{2,1,0:T(8,128)S(1)} copy-done((f32[2,256,256]{2,1,0:T(8,128)S(1)}, f32[2,256,256]{2,1,0:T(8,128)}, u32[]{:S(2)}) %copy-start.2) | copy-done | bytes 524312
  5.4 0.0 copy-start.3
  5.4 0.9 copy-done.3
  6.4 94.3 %shard_map.77 = (f32[2,256,256]{2,1,0:T(8,128)S(1)}, f32[2,256,256]{2,1,0:T(8,128)S(1)}) custom-call(s32[8]{0:T(128)S(1)} %reshape.10.off_ref, s32[1]{0:T(128)} %bitcast.1.cnt_ref, f32[2,256,256]{2,1,0:T(8,128)S(1)} %copy-done.1, f32[2,256,256]{2,1,0:T(8,128)S(1)} %copy-done.2, f32[256,256]{1,0:T(8,128)S(1)} %copy-done.3, bf16[8,256,256]{2,1,0:T(8,128)(2,1)S(1)} %copy-done), custom_call_target="tpu_custom_call" | custom-call | tf_op jit(solution)/shard_map/pallas_call | solution.py:400
  100.7 0.8 copy.13
  101.5 0.8 copy.14
Async XLA Ops:
  1.3 0.7 copy-start.4
  2.1 1.2 %copy-start = (bf16[8,256,256]{2,1,0:T(8,128)(2,1)S(1)}, bf16[8,256,256]{2,1,0:T(8,128)(2,1)}, u32[]{:S(2)}) copy-start(bf16[8,256,256]{2,1,0:T(8,128)(2,1)} %constant.2.clone.mat_ref) | copy-start | bytes 3145732
  3.4 1.0 %copy-start.1 = (f32[2,256,256]{2,1,0:T(8,128)S(1)}, f32[2,256,256]{2,1,0:T(8,128)}, u32[]{:S(2)}) copy-start(f32[2,256,256]{2,1,0:T(8,128)} %rhs_ref.1) | copy-start | bytes 1572868
  4.4 1.0 %copy-start.2 = (f32[2,256,256]{2,1,0:T(8,128)S(1)}, f32[2,256,256]{2,1,0:T(8,128)}, u32[]{:S(2)}) copy-start(f32[2,256,256]{2,1,0:T(8,128)} %probe_ref.1) | copy-start | bytes 1572868
  5.4 0.9 copy-start.3
